TPU v7x, 32 devices: a whole 2x2x4 slice. The times are simulated.
32 devices in a mesh: segment: 4 (over z), row: 4 (over y, x), col: 2 (over core).
Axes of the slice: x: 2, y: 2, z: 4, core: 2. Of those that a mesh axis runs over, the one named last changes fastest.
Arguments:
- frames: bfloat16 [2, 64, 32, 128], P(None, 'row', 'col'), may hold values from -6 to 6
- caches: bfloat16 [4, 2, 2, 64, 32, 128], P('segment', None, None, 'row', 'col'), may hold values from -5 to 5
- weights: bfloat16 [4, 2, 3, 3, 3, 128, 128], P('segment'), may hold values from -0.109375 to 0.109375
- biases: float32 [4, 2, 128], P('segment'), may hold values from -0.5 to 0.5
- gains: float32 [4, 2, 128], P('segment'), may hold values from 0.1 to 1.9
Outputs:
- sections: bfloat16 [4, 2, 64, 32, 128], P('segment', None, 'row', 'col')
All inputs are finite; a program needn't handle non-finite values.
Results may differ from a plain program's by a relative error of at most 0.0055.
Values may be sent and summed in bfloat16 or wider, within the bound.
A program may use at most 64 MiB of HBM per device.

v0:
```python
import jax
import jax.numpy as jnp
from jax import lax
from jax.sharding import PartitionSpec as P

BLOCK_FRAMES = 2


def with_halo(block, sides, width):
    for axis, dim in sides:
        count = lax.axis_size(axis)
        forward = [(i, i + 1) for i in range(count - 1)]
        backward = [(target, source) for source, target in forward]
        low = lax.ppermute(
            lax.slice_in_dim(block, block.shape[dim] - width, None, axis=dim), axis, forward
        )
        high = lax.ppermute(lax.slice_in_dim(block, 0, width, axis=dim), axis, backward)
        block = jnp.concatenate([low, block, high], axis=dim)
    return block


def shifted(value, axis, steps):
    count = lax.axis_size(axis)
    initial, last = (max(0, -steps), min(count, count - steps))
    return lax.ppermute(value, axis, [(source, source + steps) for source in range(initial, last)])


def norm_act(values, gain_row):
    values = values.astype(jnp.float32)
    scaled = (
        values * lax.rsqrt(jnp.mean(values * values, axis=-1, keepdims=True) + 1e-06) * gain_row
    )
    return jax.nn.silu(scaled).astype(jnp.bfloat16)


def convolve(padded, kernel, bias_row, piece_frames):
    tile_rows = padded.shape[1] - 2
    tile_cols = padded.shape[2] - 2
    channels = kernel.shape[-2]
    slabs = []
    for tap_t in range(3):
        for tap_h in range(3):
            for tap_w in range(3):
                slabs.append(
                    padded[
                        tap_t : tap_t + piece_frames,
                        tap_h : tap_h + tile_rows,
                        tap_w : tap_w + tile_cols,
                    ]
                )
    patches = jnp.concatenate(slabs, axis=-1)
    flat_patches = patches.reshape((piece_frames * tile_rows * tile_cols, 27 * channels))
    flat_kernel = kernel.reshape((27 * channels, kernel.shape[-1]))
    accum = jnp.dot(flat_patches, flat_kernel, preferred_element_type=jnp.float32)
    accum = accum.reshape((piece_frames, tile_rows, tile_cols, kernel.shape[-1]))
    return accum + bias_row


def window(held, fresh):
    joined = jnp.concatenate([held, fresh], axis=0)
    padded = with_halo(joined, (("row", 1), ("col", 2)), 1)
    return (padded, joined[-2:])


def on_device(frames, caches, weights, biases, gains):
    segment_index = lax.axis_index("segment")
    segment_count = lax.axis_size("segment")
    kernels = weights[0]
    offsets = biases[0]
    gain_rows = gains[0]
    piece_frames = BLOCK_FRAMES
    total_frames = frames.shape[0]
    pieces = total_frames // piece_frames
    cached = caches[0]
    held_one = cached[0]
    held_two = cached[1]
    tile_rows = frames.shape[1]
    tile_cols = frames.shape[2]
    channels = frames.shape[3]
    received = jnp.zeros((piece_frames, tile_rows, tile_cols, channels), jnp.bfloat16)
    results = jnp.zeros((total_frames, tile_rows, tile_cols, channels), jnp.bfloat16)
    empty = jnp.zeros((piece_frames, tile_rows, tile_cols, channels), jnp.float32)
    last_step = pieces + segment_count - 2
    for step_index in range(pieces + segment_count - 1):
        piece_index = step_index - segment_index
        active = (piece_index >= 0) & (piece_index < pieces)
        inputs = jnp.where(segment_index == 0, frames, received)
        normed_one = norm_act(inputs, gain_rows[0])
        window_one, next_one = window(held_one, normed_one)
        hidden = lax.cond(
            active,
            lambda window_arg: convolve(window_arg, kernels[0], offsets[0], piece_frames),
            lambda window_arg: empty,
            window_one,
        )
        normed_two = norm_act(hidden, gain_rows[1])
        window_two, next_two = window(held_two, normed_two)
        branch = lax.cond(
            active,
            lambda window_arg: convolve(window_arg, kernels[1], offsets[1], piece_frames),
            lambda window_arg: empty,
            window_two,
        )
        section_out = (inputs.astype(jnp.float32) + branch).astype(jnp.bfloat16)
        held_one = jnp.where(active, next_one, held_one)
        held_two = jnp.where(active, next_two, held_two)
        results = jnp.where(active, section_out, results)
        if step_index < last_step:
            received = shifted(section_out, "segment", 1)
    return results[None]


def solution(mesh):
    in_specs = (
        P(None, "row", "col", None),
        P("segment", None, None, "row", "col", None),
        P("segment", None, None, None, None, None, None),
        P("segment", None, None),
        P("segment", None, None),
    )
    out_specs = P("segment", None, "row", "col", None)
    return jax.shard_map(
        on_device, mesh=mesh, in_specs=in_specs, out_specs=out_specs, check_vma=False
    )
```

profile of v0, /device:TPU:25, one launch (start us, length us, event | category | flops | bytes accessed | tf_op | source)
XLA Modules:
  0.0 157.3 jit_solution(12644827177608966467)
XLA Ops:
  3.1 3.1 %collective-permute-start = (bf16[4,1,16,128]{3,2,1,0:T(8,128)(2,1)S(1)}, bf16[4,1,16,128]{3,2,1,0:T(8,128)(2,1)S(1)}, u32[]{:S(2)}, u32[]{:S(2)}) collective-permute-start(bf16[4,1,16,128]{3,2,1,0:T(8,128)(2,1)S(1)} %get-tuple-element.263), channel_id=1, source_target_pairs={{0,2},{2,4},{4,6},{1,3},{3,5},{5,7},{8,10},{10,12},{12,14},{9,11},... | collective-permute-start | bytes 49160 | tf_op jit(solution)/shard_map/ppermute | solution.py:14
  6.2 1.3 collective-permute-start.1
  7.5 3.2 %collective-permute-done.1 = bf16[4,1,16,128]{3,2,1,0:T(8,128)(2,1)S(1)} collective-permute-done((bf16[4,1,16,128]{3,2,1,0:T(8,128)(2,1)S(1)}, bf16[4,1,16,128]{3,2,1,0:T(8,128)(2,1)S(1)}, u32[]{:S(2)}, u32[]{:S(2)}) %collective-permute-start.1) | collective-permute-done | bytes 16416 | tf_op jit(solution)/shard_map/ppermute | solution.py:17
  10.8 1.3 collective-permute-start.2
  12.1 4.0 %collective-permute-start.3 = (bf16[4,18,1,128]{3,2,1,0:T(2,128)(2,1)S(1)}, bf16[4,18,1,128]{3,2,1,0:T(2,128)(2,1)S(1)}, u32[]{:S(2)}, u32[]{:S(2)}) collective-permute-start(bf16[4,18,1,128]{3,2,1,0:T(2,128)(2,1)S(1)} %get-tuple-element.248), channel_id=1, source_target_pairs={{1,0},{3,2},{5,4},{7,6},{9,8},{11,10},{13,12},{15,14},{17,16},{19,... | collective-permute-start | bytes 55304 | tf_op jit(solution)/shard_map/ppermute | solution.py:17
  18.4 4.0 %collective-permute-start.4 = (bf16[4,1,16,128]{3,2,1,0:T(8,128)(2,1)S(1)}, bf16[4,1,16,128]{3,2,1,0:T(8,128)(2,1)S(1)}, u32[]{:S(2)}, u32[]{:S(2)}) collective-permute-start(bf16[4,1,16,128]{3,2,1,0:T(8,128)(2,1)S(1)} %get-tuple-element.261), channel_id=1, source_target_pairs={{0,2},{2,4},{4,6},{1,3},{3,5},{5,7},{8,10},{10,12},{12,14},{9,11},... | collective-permute-start | bytes 49160 | tf_op jit(solution)/shard_map/ppermute | solution.py:14
  22.4 1.3 collective-permute-start.5
  23.7 3.2 %collective-permute-done.5 = bf16[4,1,16,128]{3,2,1,0:T(8,128)(2,1)S(1)} collective-permute-done((bf16[4,1,16,128]{3,2,1,0:T(8,128)(2,1)S(1)}, bf16[4,1,16,128]{3,2,1,0:T(8,128)(2,1)S(1)}, u32[]{:S(2)}, u32[]{:S(2)}) %collective-permute-start.5) | collective-permute-done | bytes 16416 | tf_op jit(solution)/shard_map/ppermute | solution.py:17
  27.0 1.3 collective-permute-start.6
  28.3 3.7 %collective-permute-start.7 = (bf16[4,18,1,128]{3,2,1,0:T(2,128)(2,1)S(1)}, bf16[4,18,1,128]{3,2,1,0:T(2,128)(2,1)S(1)}, u32[]{:S(2)}, u32[]{:S(2)}) collective-permute-start(bf16[4,18,1,128]{3,2,1,0:T(2,128)(2,1)S(1)} %get-tuple-element.246), channel_id=1, source_target_pairs={{1,0},{3,2},{5,4},{7,6},{9,8},{11,10},{13,12},{15,14},{17,16},{19,... | collective-permute-start | bytes 55304 | tf_op jit(solution)/shard_map/ppermute | solution.py:17
  34.1 1.3 collective-permute-start.8
  35.4 5.3 %collective-permute-done.8 = bf16[2,16,16,128]{3,2,1,0:T(8,128)(2,1)S(1)} collective-permute-done((bf16[2,16,16,128]{3,2,1,0:T(8,128)(2,1)S(1)}, bf16[2,16,16,128]{3,2,1,0:T(8,128)(2,1)S(1)}, u32[]{:S(2)}, u32[]{:S(2)}) %collective-permute-start.8) | collective-permute-done | bytes 131104 | tf_op jit(solution)/shard_map/ppermute | solution.py:25
  41.0 1.3 collective-permute-start.10
  42.3 4.0 %collective-permute-start.9 = (bf16[4,1,16,128]{3,2,1,0:T(8,128)(2,1)S(1)}, bf16[4,1,16,128]{3,2,1,0:T(8,128)(2,1)S(1)}, u32[]{:S(2)}, u32[]{:S(2)}) collective-permute-start(bf16[4,1,16,128]{3,2,1,0:T(8,128)(2,1)S(1)} %get-tuple-element.259), channel_id=1, source_target_pairs={{0,2},{2,4},{4,6},{1,3},{3,5},{5,7},{8,10},{10,12},{12,14},{9,11},... | collective-permute-start | bytes 49160 | tf_op jit(solution)/shard_map/ppermute | solution.py:14
  47.3 1.3 collective-permute-start.11
  48.6 4.2 %collective-permute-start.12 = (bf16[4,18,1,128]{3,2,1,0:T(2,128)(2,1)S(1)}, bf16[4,18,1,128]{3,2,1,0:T(2,128)(2,1)S(1)}, u32[]{:S(2)}, u32[]{:S(2)}) collective-permute-start(bf16[4,18,1,128]{3,2,1,0:T(2,128)(2,1)S(1)} %get-tuple-element.244), channel_id=1, source_target_pairs={{1,0},{3,2},{5,4},{7,6},{9,8},{11,10},{13,12},{15,14},{17,16},{19,... | collective-permute-start | bytes 55304 | tf_op jit(solution)/shard_map/ppermute | solution.py:17
  54.2 4.0 %collective-permute-start.13 = (bf16[4,1,16,128]{3,2,1,0:T(8,128)(2,1)S(1)}, bf16[4,1,16,128]{3,2,1,0:T(8,128)(2,1)S(1)}, u32[]{:S(2)}, u32[]{:S(2)}) collective-permute-start(bf16[4,1,16,128]{3,2,1,0:T(8,128)(2,1)S(1)} %get-tuple-element.257), channel_id=1, source_target_pairs={{0,2},{2,4},{4,6},{1,3},{3,5},{5,7},{8,10},{10,12},{12,14},{9,11},... | collective-permute-start | bytes 49160 | tf_op jit(solution)/shard_map/ppermute | solution.py:14
  58.2 1.3 collective-permute-start.14
  59.5 4.6 %collective-permute-done.14 = bf16[4,1,16,128]{3,2,1,0:T(8,128)(2,1)S(1)} collective-permute-done((bf16[4,1,16,128]{3,2,1,0:T(8,128)(2,1)S(1)}, bf16[4,1,16,128]{3,2,1,0:T(8,128)(2,1)S(1)}, u32[]{:S(2)}, u32[]{:S(2)}) %collective-permute-start.14) | collective-permute-done | bytes 16416 | tf_op jit(solution)/shard_map/ppermute | solution.py:17
  64.3 1.3 collective-permute-start.15
  65.6 3.4 %collective-permute-start.16 = (bf16[4,18,1,128]{3,2,1,0:T(2,128)(2,1)S(1)}, bf16[4,18,1,128]{3,2,1,0:T(2,128)(2,1)S(1)}, u32[]{:S(2)}, u32[]{:S(2)}) collective-permute-start(bf16[4,18,1,128]{3,2,1,0:T(2,128)(2,1)S(1)} %get-tuple-element.242), channel_id=1, source_target_pairs={{1,0},{3,2},{5,4},{7,6},{9,8},{11,10},{13,12},{15,14},{17,16},{19,... | collective-permute-start | bytes 55304 | tf_op jit(solution)/shard_map/ppermute | solution.py:17
  70.4 1.3 collective-permute-start.17
  71.7 5.3 %collective-permute-done.17 = bf16[2,16,16,128]{3,2,1,0:T(8,128)(2,1)S(1)} collective-permute-done((bf16[2,16,16,128]{3,2,1,0:T(8,128)(2,1)S(1)}, bf16[2,16,16,128]{3,2,1,0:T(8,128)(2,1)S(1)}, u32[]{:S(2)}, u32[]{:S(2)}) %collective-permute-start.17) | collective-permute-done | bytes 131104 | tf_op jit(solution)/shard_map/ppermute | solution.py:25
  77.4 4.5 %collective-permute-start.18 = (bf16[4,1,16,128]{3,2,1,0:T(8,128)(2,1)S(1)}, bf16[4,1,16,128]{3,2,1,0:T(8,128)(2,1)S(1)}, u32[]{:S(2)}, u32[]{:S(2)}) collective-permute-start(bf16[4,1,16,128]{3,2,1,0:T(8,128)(2,1)S(1)} %get-tuple-element.255), channel_id=1, source_target_pairs={{0,2},{2,4},{4,6},{1,3},{3,5},{5,7},{8,10},{10,12},{12,14},{9,11},... | collective-permute-start | bytes 49160 | tf_op jit(solution)/shard_map/ppermute | solution.py:14
  82.0 1.3 collective-permute-start.19
  83.3 3.2 %collective-permute-done.19 = bf16[4,1,16,128]{3,2,1,0:T(8,128)(2,1)S(1)} collective-permute-done((bf16[4,1,16,128]{3,2,1,0:T(8,128)(2,1)S(1)}, bf16[4,1,16,128]{3,2,1,0:T(8,128)(2,1)S(1)}, u32[]{:S(2)}, u32[]{:S(2)}) %collective-permute-start.19) | collective-permute-done | bytes 16416 | tf_op jit(solution)/shard_map/ppermute | solution.py:17
  86.6 1.3 collective-permute-start.20
  87.9 4.5 %collective-permute-start.21 = (bf16[4,18,1,128]{3,2,1,0:T(2,128)(2,1)S(1)}, bf16[4,18,1,128]{3,2,1,0:T(2,128)(2,1)S(1)}, u32[]{:S(2)}, u32[]{:S(2)}) collective-permute-start(bf16[4,18,1,128]{3,2,1,0:T(2,128)(2,1)S(1)} %get-tuple-element.240), channel_id=1, source_target_pairs={{1,0},{3,2},{5,4},{7,6},{9,8},{11,10},{13,12},{15,14},{17,16},{19,... | collective-permute-start | bytes 55304 | tf_op jit(solution)/shard_map/ppermute | solution.py:17
  93.9 2.5 %collective-permute-start.22 = (bf16[4,1,16,128]{3,2,1,0:T(8,128)(2,1)S(1)}, bf16[4,1,16,128]{3,2,1,0:T(8,128)(2,1)S(1)}, u32[]{:S(2)}, u32[]{:S(2)}) collective-permute-start(bf16[4,1,16,128]{3,2,1,0:T(8,128)(2,1)S(1)} %get-tuple-element.253), channel_id=1, source_target_pairs={{0,2},{2,4},{4,6},{1,3},{3,5},{5,7},{8,10},{10,12},{12,14},{9,11},... | collective-permute-start | bytes 49160 | tf_op jit(solution)/shard_map/ppermute | solution.py:14
  96.5 1.3 collective-permute-start.23
  97.8 3.2 %collective-permute-done.23 = bf16[4,1,16,128]{3,2,1,0:T(8,128)(2,1)S(1)} collective-permute-done((bf16[4,1,16,128]{3,2,1,0:T(8,128)(2,1)S(1)}, bf16[4,1,16,128]{3,2,1,0:T(8,128)(2,1)S(1)}, u32[]{:S(2)}, u32[]{:S(2)}) %collective-permute-start.23) | collective-permute-done | bytes 16416 | tf_op jit(solution)/shard_map/ppermute | solution.py:17
  101.1 1.3 collective-permute-start.24
  102.4 3.7 %collective-permute-start.25 = (bf16[4,18,1,128]{3,2,1,0:T(2,128)(2,1)S(1)}, bf16[4,18,1,128]{3,2,1,0:T(2,128)(2,1)S(1)}, u32[]{:S(2)}, u32[]{:S(2)}) collective-permute-start(bf16[4,18,1,128]{3,2,1,0:T(2,128)(2,1)S(1)} %get-tuple-element.238), channel_id=1, source_target_pairs={{1,0},{3,2},{5,4},{7,6},{9,8},{11,10},{13,12},{15,14},{17,16},{19,... | collective-permute-start | bytes 55304 | tf_op jit(solution)/shard_map/ppermute | solution.py:17
  108.1 1.3 collective-permute-start.26
  109.4 14.5 %collective-permute-done.26 = bf16[2,16,16,128]{3,2,1,0:T(8,128)(2,1)S(1)} collective-permute-done((bf16[2,16,16,128]{3,2,1,0:T(8,128)(2,1)S(1)}, bf16[2,16,16,128]{3,2,1,0:T(8,128)(2,1)S(1)}, u32[]{:S(2)}, u32[]{:S(2)}) %collective-permute-start.26) | collective-permute-done | bytes 131104 | tf_op jit(solution)/shard_map/ppermute | solution.py:25
  124.3 2.5 %collective-permute-start.27 = (bf16[4,1,16,128]{3,2,1,0:T(8,128)(2,1)S(1)}, bf16[4,1,16,128]{3,2,1,0:T(8,128)(2,1)S(1)}, u32[]{:S(2)}, u32[]{:S(2)}) collective-permute-start(bf16[4,1,16,128]{3,2,1,0:T(8,128)(2,1)S(1)} %get-tuple-element.251), channel_id=1, source_target_pairs={{0,2},{2,4},{4,6},{1,3},{3,5},{5,7},{8,10},{10,12},{12,14},{9,11},... | collective-permute-start | bytes 49160 | tf_op jit(solution)/shard_map/ppermute | solution.py:14
  126.8 1.3 collective-permute-start.28
  128.2 3.2 %collective-permute-done.28 = bf16[4,1,16,128]{3,2,1,0:T(8,128)(2,1)S(1)} collective-permute-done((bf16[4,1,16,128]{3,2,1,0:T(8,128)(2,1)S(1)}, bf16[4,1,16,128]{3,2,1,0:T(8,128)(2,1)S(1)}, u32[]{:S(2)}, u32[]{:S(2)}) %collective-permute-start.28) | collective-permute-done | bytes 16416 | tf_op jit(solution)/shard_map/ppermute | solution.py:17
  131.4 1.3 collective-permute-start.29
  132.7 4.3 %collective-permute-start.30 = (bf16[4,18,1,128]{3,2,1,0:T(2,128)(2,1)S(1)}, bf16[4,18,1,128]{3,2,1,0:T(2,128)(2,1)S(1)}, u32[]{:S(2)}, u32[]{:S(2)}) collective-permute-start(bf16[4,18,1,128]{3,2,1,0:T(2,128)(2,1)S(1)} %get-tuple-element.236), channel_id=1, source_target_pairs={{1,0},{3,2},{5,4},{7,6},{9,8},{11,10},{13,12},{15,14},{17,16},{19,... | collective-permute-start | bytes 55304 | tf_op jit(solution)/shard_map/ppermute | solution.py:17
  138.1 2.6 %conditional.14 = (f32[2,16,16,128]{3,2,1,0:T(8,128)S(1)}, f32[2,16,16,1]{2,1,0,3:T(8,128)S(1)}) conditional(s32[]{:T(128)} %convert_element_type.84, () %tuple.82, (bf16[4,18,18,128]{3,2,1,0:T(8,128)(2,1)S(1)}, bf16[4,18,16,128]{3,2,1,0:T(8,128)(2,1)S(1)}, bf16[4,16,16,128]{3,2,1,0:T(8,128)(2,1)S(1)}, bf16[2,16,16,128]{3,2,1,0:T(8,128)(2,1)S(1)}, ...), branch_computations={%region_19.20_spmd, %region_20.22_spmd} | conditional | flops 453180928 | bytes 13536784 | solution.py:90
  139.5 1.2 multiply_reduce_fusion.3
  140.9 2.5 %collective-permute-start.31 = (bf16[4,1,16,128]{3,2,1,0:T(8,128)(2,1)S(1)}, bf16[4,1,16,128]{3,2,1,0:T(8,128)(2,1)S(1)}, u32[]{:S(2)}, u32[]{:S(2)}) collective-permute-start(bf16[4,1,16,128]{3,2,1,0:T(8,128)(2,1)S(1)} %get-tuple-element.249), channel_id=1, source_target_pairs={{0,2},{2,4},{4,6},{1,3},{3,5},{5,7},{8,10},{10,12},{12,14},{9,11},... | collective-permute-start | bytes 49160 | tf_op jit(solution)/shard_map/ppermute | solution.py:14
  143.4 1.3 collective-permute-start.32
  144.7 3.2 %collective-permute-done.32 = bf16[4,1,16,128]{3,2,1,0:T(8,128)(2,1)S(1)} collective-permute-done((bf16[4,1,16,128]{3,2,1,0:T(8,128)(2,1)S(1)}, bf16[4,1,16,128]{3,2,1,0:T(8,128)(2,1)S(1)}, u32[]{:S(2)}, u32[]{:S(2)}) %collective-permute-start.32) | collective-permute-done | bytes 16416 | tf_op jit(solution)/shard_map/ppermute | solution.py:17
  148.0 1.3 collective-permute-start.33
  149.3 3.7 %collective-permute-start.34 = (bf16[4,18,1,128]{3,2,1,0:T(2,128)(2,1)S(1)}, bf16[4,18,1,128]{3,2,1,0:T(2,128)(2,1)S(1)}, u32[]{:S(2)}, u32[]{:S(2)}) collective-permute-start(bf16[4,18,1,128]{3,2,1,0:T(2,128)(2,1)S(1)} %get-tuple-element.234), channel_id=1, source_target_pairs={{1,0},{3,2},{5,4},{7,6},{9,8},{11,10},{13,12},{15,14},{17,16},{19,... | collective-permute-start | bytes 55304 | tf_op jit(solution)/shard_map/ppermute | solution.py:17
  154.1 2.5 %conditional.15 = (f32[2,16,16,128]{3,2,1,0:T(8,128)S(1)}) conditional(s32[]{:T(128)} %convert_element_type.84, () %tuple.81, (bf16[4,18,18,128]{3,2,1,0:T(8,128)(2,1)S(1)}, bf16[4,18,16,128]{3,2,1,0:T(8,128)(2,1)S(1)}, bf16[4,16,16,128]{3,2,1,0:T(8,128)(2,1)S(1)}, bf16[2,16,16,128]{3,2,1,0:T(8,128)(2,1)S(1)}, ...), branch_computations={%region_22.23_spmd, %region_23.24_spmd} | conditional | flops 453050368 | bytes 13534728 | solution.py:98
  (177 shorter events, 22.8 us)
Async XLA Ops:
  0.0 17.2 %copy-start = (bf16[1,2,3,3,3,128,128]{6,5,4,3,2,1,0:T(8,128)(2,1)S(1)}, bf16[1,2,3,3,3,128,128]{6,5,4,3,2,1,0:T(8,128)(2,1)}, u32[]{:S(2)}) copy-start(bf16[1,2,3,3,3,128,128]{6,5,4,3,2,1,0:T(8,128)(2,1)} %param.23) | copy-start | bytes 5308420
  0.0 17.2 %copy-start.5 = (f32[1,2,128]{2,1,0:T(2,128)S(1)}, f32[1,2,128]{2,1,0:T(2,128)}, u32[]{:S(2)}) copy-start(f32[1,2,128]{2,1,0:T(2,128)} %param.24) | copy-start | bytes 3076
  3.1 4.4 %collective-permute-start = (bf16[4,1,16,128]{3,2,1,0:T(8,128)(2,1)S(1)}, bf16[4,1,16,128]{3,2,1,0:T(8,128)(2,1)S(1)}, u32[]{:S(2)}, u32[]{:S(2)}) collective-permute-start(bf16[4,1,16,128]{3,2,1,0:T(8,128)(2,1)S(1)} %get-tuple-element.263), channel_id=1, source_target_pairs={{0,2},{2,4},{4,6},{1,3},{3,5},{5,7},{8,10},{10,12},{12,14},{9,11},... | collective-permute-start | bytes 49160 | tf_op jit(solution)/shard_map/ppermute | solution.py:14
  6.2 4.5 %collective-permute-start.1 = (bf16[4,1,16,128]{3,2,1,0:T(8,128)(2,1)S(1)}, bf16[4,1,16,128]{3,2,1,0:T(8,128)(2,1)S(1)}, u32[]{:S(2)}, u32[]{:S(2)}) collective-permute-start(bf16[4,1,16,128]{3,2,1,0:T(8,128)(2,1)S(1)} %get-tuple-element.264), channel_id=1, source_target_pairs={{2,0},{4,2},{6,4},{3,1},{5,3},{7,5},{10,8},{12,10},{14,12},{11,9},... | collective-permute-start | bytes 49160 | tf_op jit(solution)/shard_map/ppermute | solution.py:17
  10.8 5.4 %collective-permute-start.2 = (bf16[4,18,1,128]{3,2,1,0:T(2,128)(2,1)S(1)}, bf16[4,18,1,128]{3,2,1,0:T(2,128)(2,1)S(1)}, u32[]{:S(2)}, u32[]{:S(2)}) collective-permute-start(bf16[4,18,1,128]{3,2,1,0:T(2,128)(2,1)S(1)} %get-tuple-element.247), channel_id=1, source_target_pairs={{0,1},{2,3},{4,5},{6,7},{8,9},{10,11},{12,13},{14,15},{16,17},{18,... | collective-permute-start | bytes 55304 | tf_op jit(solution)/shard_map/ppermute | solution.py:14
  12.1 4.9 %collective-permute-start.3 = (bf16[4,18,1,128]{3,2,1,0:T(2,128)(2,1)S(1)}, bf16[4,18,1,128]{3,2,1,0:T(2,128)(2,1)S(1)}, u32[]{:S(2)}, u32[]{:S(2)}) collective-permute-start(bf16[4,18,1,128]{3,2,1,0:T(2,128)(2,1)S(1)} %get-tuple-element.248), channel_id=1, source_target_pairs={{1,0},{3,2},{5,4},{7,6},{9,8},{11,10},{13,12},{15,14},{17,16},{19,... | collective-permute-start | bytes 55304 | tf_op jit(solution)/shard_map/ppermute | solution.py:17
  17.3 1.0 copy-start.4
  18.4 5.3 %collective-permute-start.4 = (bf16[4,1,16,128]{3,2,1,0:T(8,128)(2,1)S(1)}, bf16[4,1,16,128]{3,2,1,0:T(8,128)(2,1)S(1)}, u32[]{:S(2)}, u32[]{:S(2)}) collective-permute-start(bf16[4,1,16,128]{3,2,1,0:T(8,128)(2,1)S(1)} %get-tuple-element.261), channel_id=1, source_target_pairs={{0,2},{2,4},{4,6},{1,3},{3,5},{5,7},{8,10},{10,12},{12,14},{9,11},... | collective-permute-start | bytes 49160 | tf_op jit(solution)/shard_map/ppermute | solution.py:14
  22.4 4.5 %collective-permute-start.5 = (bf16[4,1,16,128]{3,2,1,0:T(8,128)(2,1)S(1)}, bf16[4,1,16,128]{3,2,1,0:T(8,128)(2,1)S(1)}, u32[]{:S(2)}, u32[]{:S(2)}) collective-permute-start(bf16[4,1,16,128]{3,2,1,0:T(8,128)(2,1)S(1)} %get-tuple-element.262), channel_id=1, source_target_pairs={{2,0},{4,2},{6,4},{3,1},{5,3},{7,5},{10,8},{12,10},{14,12},{11,9},... | collective-permute-start | bytes 49160 | tf_op jit(solution)/shard_map/ppermute | solution.py:17
  27.0 5.0 %collective-permute-start.6 = (bf16[4,18,1,128]{3,2,1,0:T(2,128)(2,1)S(1)}, bf16[4,18,1,128]{3,2,1,0:T(2,128)(2,1)S(1)}, u32[]{:S(2)}, u32[]{:S(2)}) collective-permute-start(bf16[4,18,1,128]{3,2,1,0:T(2,128)(2,1)S(1)} %get-tuple-element.245), channel_id=1, source_target_pairs={{0,1},{2,3},{4,5},{6,7},{8,9},{10,11},{12,13},{14,15},{16,17},{18,... | collective-permute-start | bytes 55304 | tf_op jit(solution)/shard_map/ppermute | solution.py:14
  28.3 4.5 %collective-permute-start.7 = (bf16[4,18,1,128]{3,2,1,0:T(2,128)(2,1)S(1)}, bf16[4,18,1,128]{3,2,1,0:T(2,128)(2,1)S(1)}, u32[]{:S(2)}, u32[]{:S(2)}) collective-permute-start(bf16[4,18,1,128]{3,2,1,0:T(2,128)(2,1)S(1)} %get-tuple-element.246), channel_id=1, source_target_pairs={{1,0},{3,2},{5,4},{7,6},{9,8},{11,10},{13,12},{15,14},{17,16},{19,... | collective-permute-start | bytes 55304 | tf_op jit(solution)/shard_map/ppermute | solution.py:17
  33.1 0.9 copy-start.1
  34.1 6.6 %collective-permute-start.8 = (bf16[2,16,16,128]{3,2,1,0:T(8,128)(2,1)S(1)}, bf16[2,16,16,128]{3,2,1,0:T(8,128)(2,1)S(1)}, u32[]{:S(2)}, u32[]{:S(2)}) collective-permute-start(bf16[2,16,16,128]{3,2,1,0:T(8,128)(2,1)S(1)} %fusion.8), channel_id=1, source_target_pairs={{0,8},{8,16},{16,24},{1,9},{9,17},{17,25},{2,10},{10,18},{18,26},{... | collective-permute-start | bytes 393224 | tf_op jit(solution)/shard_map/ppermute | solution.py:25
  41.0 5.3 %collective-permute-start.10 = (bf16[4,1,16,128]{3,2,1,0:T(8,128)(2,1)S(1)}, bf16[4,1,16,128]{3,2,1,0:T(8,128)(2,1)S(1)}, u32[]{:S(2)}, u32[]{:S(2)}) collective-permute-start(bf16[4,1,16,128]{3,2,1,0:T(8,128)(2,1)S(1)} %get-tuple-element.260), channel_id=1, source_target_pairs={{2,0},{4,2},{6,4},{3,1},{5,3},{7,5},{10,8},{12,10},{14,12},{11,9},... | collective-permute-start | bytes 49160 | tf_op jit(solution)/shard_map/ppermute | solution.py:17
  42.3 4.8 %collective-permute-start.9 = (bf16[4,1,16,128]{3,2,1,0:T(8,128)(2,1)S(1)}, bf16[4,1,16,128]{3,2,1,0:T(8,128)(2,1)S(1)}, u32[]{:S(2)}, u32[]{:S(2)}) collective-permute-start(bf16[4,1,16,128]{3,2,1,0:T(8,128)(2,1)S(1)} %get-tuple-element.259), channel_id=1, source_target_pairs={{0,2},{2,4},{4,6},{1,3},{3,5},{5,7},{8,10},{10,12},{12,14},{9,11},... | collective-permute-start | bytes 49160 | tf_op jit(solution)/shard_map/ppermute | solution.py:14
  47.3 5.6 %collective-permute-start.11 = (bf16[4,18,1,128]{3,2,1,0:T(2,128)(2,1)S(1)}, bf16[4,18,1,128]{3,2,1,0:T(2,128)(2,1)S(1)}, u32[]{:S(2)}, u32[]{:S(2)}) collective-permute-start(bf16[4,18,1,128]{3,2,1,0:T(2,128)(2,1)S(1)} %get-tuple-element.243), channel_id=1, source_target_pairs={{0,1},{2,3},{4,5},{6,7},{8,9},{10,11},{12,13},{14,15},{16,17},{18,... | collective-permute-start | bytes 55304 | tf_op jit(solution)/shard_map/ppermute | solution.py:14
  48.6 5.1 %collective-permute-start.12 = (bf16[4,18,1,128]{3,2,1,0:T(2,128)(2,1)S(1)}, bf16[4,18,1,128]{3,2,1,0:T(2,128)(2,1)S(1)}, u32[]{:S(2)}, u32[]{:S(2)}) collective-permute-start(bf16[4,18,1,128]{3,2,1,0:T(2,128)(2,1)S(1)} %get-tuple-element.244), channel_id=1, source_target_pairs={{1,0},{3,2},{5,4},{7,6},{9,8},{11,10},{13,12},{15,14},{17,16},{19,... | collective-permute-start | bytes 55304 | tf_op jit(solution)/shard_map/ppermute | solution.py:17
  54.2 5.3 %collective-permute-start.13 = (bf16[4,1,16,128]{3,2,1,0:T(8,128)(2,1)S(1)}, bf16[4,1,16,128]{3,2,1,0:T(8,128)(2,1)S(1)}, u32[]{:S(2)}, u32[]{:S(2)}) collective-permute-start(bf16[4,1,16,128]{3,2,1,0:T(8,128)(2,1)S(1)} %get-tuple-element.257), channel_id=1, source_target_pairs={{0,2},{2,4},{4,6},{1,3},{3,5},{5,7},{8,10},{10,12},{12,14},{9,11},... | collective-permute-start | bytes 49160 | tf_op jit(solution)/shard_map/ppermute | solution.py:14
  58.2 5.9 %collective-permute-start.14 = (bf16[4,1,16,128]{3,2,1,0:T(8,128)(2,1)S(1)}, bf16[4,1,16,128]{3,2,1,0:T(8,128)(2,1)S(1)}, u32[]{:S(2)}, u32[]{:S(2)}) collective-permute-start(bf16[4,1,16,128]{3,2,1,0:T(8,128)(2,1)S(1)} %get-tuple-element.258), channel_id=1, source_target_pairs={{2,0},{4,2},{6,4},{3,1},{5,3},{7,5},{10,8},{12,10},{14,12},{11,9},... | collective-permute-start | bytes 49160 | tf_op jit(solution)/shard_map/ppermute | solution.py:17
  64.3 4.7 %collective-permute-start.15 = (bf16[4,18,1,128]{3,2,1,0:T(2,128)(2,1)S(1)}, bf16[4,18,1,128]{3,2,1,0:T(2,128)(2,1)S(1)}, u32[]{:S(2)}, u32[]{:S(2)}) collective-permute-start(bf16[4,18,1,128]{3,2,1,0:T(2,128)(2,1)S(1)} %get-tuple-element.241), channel_id=1, source_target_pairs={{0,1},{2,3},{4,5},{6,7},{8,9},{10,11},{12,13},{14,15},{16,17},{18,... | collective-permute-start | bytes 55304 | tf_op jit(solution)/shard_map/ppermute | solution.py:14
  65.6 4.3 %collective-permute-start.16 = (bf16[4,18,1,128]{3,2,1,0:T(2,128)(2,1)S(1)}, bf16[4,18,1,128]{3,2,1,0:T(2,128)(2,1)S(1)}, u32[]{:S(2)}, u32[]{:S(2)}) collective-permute-start(bf16[4,18,1,128]{3,2,1,0:T(2,128)(2,1)S(1)} %get-tuple-element.242), channel_id=1, source_target_pairs={{1,0},{3,2},{5,4},{7,6},{9,8},{11,10},{13,12},{15,14},{17,16},{19,... | collective-permute-start | bytes 55304 | tf_op jit(solution)/shard_map/ppermute | solution.py:17
  70.4 6.6 %collective-permute-start.17 = (bf16[2,16,16,128]{3,2,1,0:T(8,128)(2,1)S(1)}, bf16[2,16,16,128]{3,2,1,0:T(8,128)(2,1)S(1)}, u32[]{:S(2)}, u32[]{:S(2)}) collective-permute-start(bf16[2,16,16,128]{3,2,1,0:T(8,128)(2,1)S(1)} %fusion.17), channel_id=1, source_target_pairs={{0,8},{8,16},{16,24},{1,9},{9,17},{17,25},{2,10},{10,18},{18,26},{... | collective-permute-start | bytes 393224 | tf_op jit(solution)/shard_map/ppermute | solution.py:25
  77.1 6.2 %copy-start.2 = (bf16[2,16,16,128]{3,2,1,0:T(8,128)(2,1)}, bf16[2,16,16,128]{3,2,1,0:T(8,128)(2,1)S(1)}, u32[]{:S(2)}) copy-start(bf16[2,16,16,128]{3,2,1,0:T(8,128)(2,1)S(1)} %get-tuple-element.218) | copy-start | bytes 393220
  77.4 5.9 %collective-permute-start.18 = (bf16[4,1,16,128]{3,2,1,0:T(8,128)(2,1)S(1)}, bf16[4,1,16,128]{3,2,1,0:T(8,128)(2,1)S(1)}, u32[]{:S(2)}, u32[]{:S(2)}) collective-permute-start(bf16[4,1,16,128]{3,2,1,0:T(8,128)(2,1)S(1)} %get-tuple-element.255), channel_id=1, source_target_pairs={{0,2},{2,4},{4,6},{1,3},{3,5},{5,7},{8,10},{10,12},{12,14},{9,11},... | collective-permute-start | bytes 49160 | tf_op jit(solution)/shard_map/ppermute | solution.py:14
  82.0 4.5 %collective-permute-start.19 = (bf16[4,1,16,128]{3,2,1,0:T(8,128)(2,1)S(1)}, bf16[4,1,16,128]{3,2,1,0:T(8,128)(2,1)S(1)}, u32[]{:S(2)}, u32[]{:S(2)}) collective-permute-start(bf16[4,1,16,128]{3,2,1,0:T(8,128)(2,1)S(1)} %get-tuple-element.256), channel_id=1, source_target_pairs={{2,0},{4,2},{6,4},{3,1},{5,3},{7,5},{10,8},{12,10},{14,12},{11,9},... | collective-permute-start | bytes 49160 | tf_op jit(solution)/shard_map/ppermute | solution.py:17
  86.6 5.9 %collective-permute-start.20 = (bf16[4,18,1,128]{3,2,1,0:T(2,128)(2,1)S(1)}, bf16[4,18,1,128]{3,2,1,0:T(2,128)(2,1)S(1)}, u32[]{:S(2)}, u32[]{:S(2)}) collective-permute-start(bf16[4,18,1,128]{3,2,1,0:T(2,128)(2,1)S(1)} %get-tuple-element.239), channel_id=1, source_target_pairs={{0,1},{2,3},{4,5},{6,7},{8,9},{10,11},{12,13},{14,15},{16,17},{18,... | collective-permute-start | bytes 55304 | tf_op jit(solution)/shard_map/ppermute | solution.py:14
  87.9 5.4 %collective-permute-start.21 = (bf16[4,18,1,128]{3,2,1,0:T(2,128)(2,1)S(1)}, bf16[4,18,1,128]{3,2,1,0:T(2,128)(2,1)S(1)}, u32[]{:S(2)}, u32[]{:S(2)}) collective-permute-start(bf16[4,18,1,128]{3,2,1,0:T(2,128)(2,1)S(1)} %get-tuple-element.240), channel_id=1, source_target_pairs={{1,0},{3,2},{5,4},{7,6},{9,8},{11,10},{13,12},{15,14},{17,16},{19,... | collective-permute-start | bytes 55304 | tf_op jit(solution)/shard_map/ppermute | solution.py:17
  93.9 3.9 %collective-permute-start.22 = (bf16[4,1,16,128]{3,2,1,0:T(8,128)(2,1)S(1)}, bf16[4,1,16,128]{3,2,1,0:T(8,128)(2,1)S(1)}, u32[]{:S(2)}, u32[]{:S(2)}) collective-permute-start(bf16[4,1,16,128]{3,2,1,0:T(8,128)(2,1)S(1)} %get-tuple-element.253), channel_id=1, source_target_pairs={{0,2},{2,4},{4,6},{1,3},{3,5},{5,7},{8,10},{10,12},{12,14},{9,11},... | collective-permute-start | bytes 49160 | tf_op jit(solution)/shard_map/ppermute | solution.py:14
  96.5 4.5 %collective-permute-start.23 = (bf16[4,1,16,128]{3,2,1,0:T(8,128)(2,1)S(1)}, bf16[4,1,16,128]{3,2,1,0:T(8,128)(2,1)S(1)}, u32[]{:S(2)}, u32[]{:S(2)}) collective-permute-start(bf16[4,1,16,128]{3,2,1,0:T(8,128)(2,1)S(1)} %get-tuple-element.254), channel_id=1, source_target_pairs={{2,0},{4,2},{6,4},{3,1},{5,3},{7,5},{10,8},{12,10},{14,12},{11,9},... | collective-permute-start | bytes 49160 | tf_op jit(solution)/shard_map/ppermute | solution.py:17
  101.1 5.0 %collective-permute-start.24 = (bf16[4,18,1,128]{3,2,1,0:T(2,128)(2,1)S(1)}, bf16[4,18,1,128]{3,2,1,0:T(2,128)(2,1)S(1)}, u32[]{:S(2)}, u32[]{:S(2)}) collective-permute-start(bf16[4,18,1,128]{3,2,1,0:T(2,128)(2,1)S(1)} %get-tuple-element.237), channel_id=1, source_target_pairs={{0,1},{2,3},{4,5},{6,7},{8,9},{10,11},{12,13},{14,15},{16,17},{18,... | collective-permute-start | bytes 55304 | tf_op jit(solution)/shard_map/ppermute | solution.py:14
  102.4 4.5 %collective-permute-start.25 = (bf16[4,18,1,128]{3,2,1,0:T(2,128)(2,1)S(1)}, bf16[4,18,1,128]{3,2,1,0:T(2,128)(2,1)S(1)}, u32[]{:S(2)}, u32[]{:S(2)}) collective-permute-start(bf16[4,18,1,128]{3,2,1,0:T(2,128)(2,1)S(1)} %get-tuple-element.238), channel_id=1, source_target_pairs={{1,0},{3,2},{5,4},{7,6},{9,8},{11,10},{13,12},{15,14},{17,16},{19,... | collective-permute-start | bytes 55304 | tf_op jit(solution)/shard_map/ppermute | solution.py:17
  107.2 0.9 copy-start.3
  108.1 15.8 %collective-permute-start.26 = (bf16[2,16,16,128]{3,2,1,0:T(8,128)(2,1)S(1)}, bf16[2,16,16,128]{3,2,1,0:T(8,128)(2,1)S(1)}, u32[]{:S(2)}, u32[]{:S(2)}) collective-permute-start(bf16[2,16,16,128]{3,2,1,0:T(8,128)(2,1)S(1)} %fusion.26), channel_id=1, source_target_pairs={{0,8},{8,16},{16,24},{1,9},{9,17},{17,25},{2,10},{10,18},{18,26},{... | collective-permute-start | bytes 393224 | tf_op jit(solution)/shard_map/ppermute | solution.py:25
  124.3 3.9 %collective-permute-start.27 = (bf16[4,1,16,128]{3,2,1,0:T(8,128)(2,1)S(1)}, bf16[4,1,16,128]{3,2,1,0:T(8,128)(2,1)S(1)}, u32[]{:S(2)}, u32[]{:S(2)}) collective-permute-start(bf16[4,1,16,128]{3,2,1,0:T(8,128)(2,1)S(1)} %get-tuple-element.251), channel_id=1, source_target_pairs={{0,2},{2,4},{4,6},{1,3},{3,5},{5,7},{8,10},{10,12},{12,14},{9,11},... | collective-permute-start | bytes 49160 | tf_op jit(solution)/shard_map/ppermute | solution.py:14
  126.8 4.5 %collective-permute-start.28 = (bf16[4,1,16,128]{3,2,1,0:T(8,128)(2,1)S(1)}, bf16[4,1,16,128]{3,2,1,0:T(8,128)(2,1)S(1)}, u32[]{:S(2)}, u32[]{:S(2)}) collective-permute-start(bf16[4,1,16,128]{3,2,1,0:T(8,128)(2,1)S(1)} %get-tuple-element.252), channel_id=1, source_target_pairs={{2,0},{4,2},{6,4},{3,1},{5,3},{7,5},{10,8},{12,10},{14,12},{11,9},... | collective-permute-start | bytes 49160 | tf_op jit(solution)/shard_map/ppermute | solution.py:17
  131.4 5.6 %collective-permute-start.29 = (bf16[4,18,1,128]{3,2,1,0:T(2,128)(2,1)S(1)}, bf16[4,18,1,128]{3,2,1,0:T(2,128)(2,1)S(1)}, u32[]{:S(2)}, u32[]{:S(2)}) collective-permute-start(bf16[4,18,1,128]{3,2,1,0:T(2,128)(2,1)S(1)} %get-tuple-element.235), channel_id=1, source_target_pairs={{0,1},{2,3},{4,5},{6,7},{8,9},{10,11},{12,13},{14,15},{16,17},{18,... | collective-permute-start | bytes 55304 | tf_op jit(solution)/shard_map/ppermute | solution.py:14
  132.7 5.1 %collective-permute-start.30 = (bf16[4,18,1,128]{3,2,1,0:T(2,128)(2,1)S(1)}, bf16[4,18,1,128]{3,2,1,0:T(2,128)(2,1)S(1)}, u32[]{:S(2)}, u32[]{:S(2)}) collective-permute-start(bf16[4,18,1,128]{3,2,1,0:T(2,128)(2,1)S(1)} %get-tuple-element.236), channel_id=1, source_target_pairs={{1,0},{3,2},{5,4},{7,6},{9,8},{11,10},{13,12},{15,14},{17,16},{19,... | collective-permute-start | bytes 55304 | tf_op jit(solution)/shard_map/ppermute | solution.py:17
  140.9 3.9 %collective-permute-start.31 = (bf16[4,1,16,128]{3,2,1,0:T(8,128)(2,1)S(1)}, bf16[4,1,16,128]{3,2,1,0:T(8,128)(2,1)S(1)}, u32[]{:S(2)}, u32[]{:S(2)}) collective-permute-start(bf16[4,1,16,128]{3,2,1,0:T(8,128)(2,1)S(1)} %get-tuple-element.249), channel_id=1, source_target_pairs={{0,2},{2,4},{4,6},{1,3},{3,5},{5,7},{8,10},{10,12},{12,14},{9,11},... | collective-permute-start | bytes 49160 | tf_op jit(solution)/shard_map/ppermute | solution.py:14
  143.4 4.5 %collective-permute-start.32 = (bf16[4,1,16,128]{3,2,1,0:T(8,128)(2,1)S(1)}, bf16[4,1,16,128]{3,2,1,0:T(8,128)(2,1)S(1)}, u32[]{:S(2)}, u32[]{:S(2)}) collective-permute-start(bf16[4,1,16,128]{3,2,1,0:T(8,128)(2,1)S(1)} %get-tuple-element.250), channel_id=1, source_target_pairs={{2,0},{4,2},{6,4},{3,1},{5,3},{7,5},{10,8},{12,10},{14,12},{11,9},... | collective-permute-start | bytes 49160 | tf_op jit(solution)/shard_map/ppermute | solution.py:17
  148.0 5.0 %collective-permute-start.33 = (bf16[4,18,1,128]{3,2,1,0:T(2,128)(2,1)S(1)}, bf16[4,18,1,128]{3,2,1,0:T(2,128)(2,1)S(1)}, u32[]{:S(2)}, u32[]{:S(2)}) collective-permute-start(bf16[4,18,1,128]{3,2,1,0:T(2,128)(2,1)S(1)} %get-tuple-element.233), channel_id=1, source_target_pairs={{0,1},{2,3},{4,5},{6,7},{8,9},{10,11},{12,13},{14,15},{16,17},{18,... | collective-permute-start | bytes 55304 | tf_op jit(solution)/shard_map/ppermute | solution.py:14
  149.3 4.5 %collective-permute-start.34 = (bf16[4,18,1,128]{3,2,1,0:T(2,128)(2,1)S(1)}, bf16[4,18,1,128]{3,2,1,0:T(2,128)(2,1)S(1)}, u32[]{:S(2)}, u32[]{:S(2)}) collective-permute-start(bf16[4,18,1,128]{3,2,1,0:T(2,128)(2,1)S(1)} %get-tuple-element.234), channel_id=1, source_target_pairs={{1,0},{3,2},{5,4},{7,6},{9,8},{11,10},{13,12},{15,14},{17,16},{19,... | collective-permute-start | bytes 55304 | tf_op jit(solution)/shard_map/ppermute | solution.py:17
where the time goes:
time: 158 us; the launch traced here: 157 us
  starting transfers between devices  83.4 us (53%)
  waiting for transfers between devices  56.1 us (36%)
  local copies, waits for them, and re-layouts  7.4 us (5%)
  other arithmetic  6.55 us (4%)
  matrix products  2.24 us (1%)
    ppermute x16, starting transfers between devices, with_halo(): lax.ppermute(lax.slice_in_dim(block, 0, width, axis=dim), axis, backward)  41.9 us
    ppermute x16, starting transfers between devices, with_halo(): lax.ppermute(lax.slice_in_dim(block, block.shape[dim] - width, None, axis...  37.6 us
    ppermute x16, waiting for transfers between devices, with_halo(): lax.ppermute(lax.slice_in_dim(block, 0, width, axis=dim), axis, backward)  30.1 us
    ppermute x3, waiting for transfers between devices, shifted(): lax.ppermute(value, axis, [(source, source + steps) for source in range(i...  25.1 us
    ppermute x3, starting transfers between devices, shifted(): lax.ppermute(value, axis, [(source, source + steps) for source in range(i...  3.88 us
  transfers between devices with their start and end apart: 35, of which 19 were waited for; matrix products, arithmetic and copies ran while one was open for 0% of the time, Pallas kernels for 0%

commit v1 on v0

v1 whole, which is shorter than its diff:
```python
import functools

import jax
import jax.numpy as jnp
from jax import lax
from jax.experimental import pallas as pl
from jax.experimental.pallas import tpu as pltpu
from jax.sharding import PartitionSpec as P

STRIP = 8
TAPS = 3
AROUND = [(dr, dc) for dr in (-1, 0, 1) for dc in (-1, 0, 1)]
CENTRE = AROUND.index((0, 0))


def divisor(count, most):
    return max(d for d in range(1, most + 1) if count % d == 0)


def source_range(step, size, width):
    return pl.ds(0, size) if step == 0 else pl.ds(0 if step < 0 else size - width, width)


def target_range(step, size, width, edge):
    if step == 0:
        return pl.ds(edge, size)
    return pl.ds(edge + size, width) if step < 0 else pl.ds(edge - width, width)


def norm_act(values, gain_row):
    scale = lax.rsqrt(jnp.mean(values * values, axis=-1, keepdims=True) + 1e-06)
    half = 0.5 * (values * scale * gain_row)
    return half * jnp.tanh(half) + half


def put_taps(store, start, values):
    size, channels = values.shape
    rows = pl.ds(start, size)
    store[rows, 0:channels] = pltpu.roll(values, 1, 0).astype(jnp.bfloat16)
    store[rows, channels : 2 * channels] = values.astype(jnp.bfloat16)
    store[rows, 2 * channels : 3 * channels] = pltpu.roll(values, size - 1, 0).astype(jnp.bfloat16)


def kernel(
    counts,
    frames, caches, weights, biases, gains,
    out,
    x_pad, one_pad, two_pad, taps_one, taps_two, sum_one, sum_two, inside,
    send_sem, recv_sem, local_sem,
):
    segments, tile_rows_n, tile_cols_n = counts
    seg, row, col = (lax.axis_index(name) for name in ("segment", "row", "col"))
    total, rows, cols, channels = frames.shape
    pitch = x_pad.shape[2]

    def exists(dr, dc):
        r, c = row + dr, col + dc
        return (r >= 0) & (r < tile_rows_n) & (c >= 0) & (c < tile_cols_n)

    def device(dz, dr, dc):
        return {"segment": seg + dz, "row": row + dr, "col": col + dc}

    def remote(source, target, halo, send_group, recv_group, dz, which):
        dr, dc = AROUND[which]
        src_r, src_c = source_range(dr, rows, halo), source_range(dc, cols, STRIP)
        dst_r, dst_c = target_range(dr, rows, halo, halo), target_range(dc, cols, STRIP, STRIP)
        lead = (slice(None),) * (len(source.shape) - 3)
        return pltpu.make_async_remote_copy(
            src_ref=source.at[lead + (src_r, src_c)],
            dst_ref=target.at[lead + (dst_r, dst_c)],
            send_sem=send_sem.at[send_group, which],
            recv_sem=recv_sem.at[recv_group, which],
            device_id=device(dz, dr, dc),
            device_id_type=pl.DeviceIdType.MESH,
        )

    streams = [
        (caches.at[0], one_pad, 2, 0, 0, 0),
        (caches.at[1], two_pad, 1, 1, 1, 0),
    ] + [(frames.at[f], x_pad.at[f], 2, 2 + f, 2 + f, 0) for f in range(total)]
    onward = [(out.at[f], x_pad.at[f], 2, 2 + total + f, 2 + f, 1) for f in range(total)]

    def each(stream, allowed, action):
        for which, (dr, dc) in enumerate(AROUND):
            if stream[5] == 0 and which == CENTRE:
                continue
            good = exists(dr, dc) if action != "recv" else exists(-dr, -dc)
            if allowed is not None:
                good = good & allowed

            @pl.when(good)
            def _():
                copy = remote(*stream, which)
                if action == "start":
                    copy.start()
                elif action == "send":
                    copy.wait_send()
                else:
                    copy.wait_recv()

    for pad, halo in ((x_pad, 2), (one_pad, 2), (two_pad, 1)):
        count = pad.shape[0]
        side = pitch - STRIP - cols
        pad[:, 0:halo] = jnp.zeros((count, halo, pitch, channels), pad.dtype)
        pad[:, halo + rows :] = jnp.zeros((count, halo, pitch, channels), pad.dtype)
        pad[:, halo : halo + rows, 0:STRIP] = jnp.zeros((count, rows, STRIP, channels), pad.dtype)
        pad[:, halo : halo + rows, STRIP + cols :] = jnp.zeros((count, rows, side, channels), pad.dtype)

    barrier = pltpu.get_barrier_semaphore()
    arrivals = 0
    for dz in (-1, 0, 1):
        for dr, dc in AROUND:
            if (dz, dr, dc) == (0, 0, 0):
                continue
            good = exists(dr, dc) & (seg + dz >= 0) & (seg + dz < segments)

            @pl.when(good)
            def _():
                pl.semaphore_signal(
                    barrier, inc=1, device_id=device(dz, dr, dc),
                    device_id_type=pl.DeviceIdType.MESH,
                )

            arrivals = arrivals + good.astype(jnp.int32)
    centre_of = lambda pad, halo: pad.at[:, pl.ds(halo, rows), pl.ds(STRIP, cols)]
    local = [
        pltpu.make_async_copy(caches.at[0], centre_of(one_pad, 2), local_sem.at[0]),
        pltpu.make_async_copy(caches.at[1], centre_of(two_pad, 1), local_sem.at[1]),
    ]
    own = pltpu.make_async_copy(frames, centre_of(x_pad, 2), local_sem.at[2])
    for copy in local:
        copy.start()
    first = seg == 0
    later = seg > 0
    more = seg < segments - 1

    @pl.when(first)
    def _():
        own.start()

    pl.semaphore_wait(barrier, arrivals)

    each(streams[0], None, "start")
    for f in range(total):
        each(streams[2 + f], first, "start")
    each(streams[1], None, "start")

    cell = lax.broadcasted_iota(jnp.int32, inside.shape, 0)
    cell_row = row * rows + cell // pitch - 1
    cell_col = col * cols + cell % pitch - STRIP
    inside[...] = jnp.where(
        (cell_row >= 0) & (cell_row < rows * tile_rows_n)
        & (cell_col >= 0) & (cell_col < cols * tile_cols_n), 1.0, 0.0,
    )

    def kernel_of(which, *times):
        return jnp.concatenate([weights[which, t] for t in times], axis=1)

    def product(store, start, size, matrix):
        patches = jnp.concatenate(
            [store[pl.ds((start + dh) * pitch, size * pitch), :] for dh in range(TAPS)], axis=1
        )
        return jnp.dot(patches, matrix, preferred_element_type=jnp.float32)

    step_in = divisor(rows + 4, 5)
    step_one = divisor(rows + 2, 6)
    step_two = divisor(rows, 4)

    def load_taps(pad, index, store, size, step, transform):
        for start in range(0, size, step):
            values = pad[index, start : start + step].reshape(step * pitch, channels)
            put_taps(store, start * pitch, transform(values.astype(jnp.float32)))

    def cached(which, pad, store, sums, size, step, tall):
        bias = biases[which : which + 1]
        load_taps(pad, 0, store, tall, divisor(tall, 5), lambda v: v)
        for start in range(0, size, step):
            part = pl.ds(start * pitch, step * pitch)
            sums[0, part] = product(store, start, step, kernel_of(which, 0)) + bias
        load_taps(pad, 1, store, tall, divisor(tall, 5), lambda v: v)
        for start in range(0, size, step):
            part = pl.ds(start * pitch, step * pitch)
            both = product(store, start, step, kernel_of(which, 1, 0))
            sums[0, part] += both[:, :channels]
            sums[1, part] = both[:, channels:] + bias

    local[0].wait()
    each(streams[0], None, "recv")
    cached(0, one_pad, taps_one, sum_one, rows + 2, step_one, rows + 4)
    local[1].wait()
    each(streams[1], None, "recv")
    cached(1, two_pad, taps_two, sum_two, rows, step_two, rows + 2)

    @pl.when(first)
    def _():
        own.wait()

    for f in range(total):
        each(streams[2 + f], first, "recv")
        each(onward[f], later, "recv")
        load_taps(x_pad, f, taps_one, rows + 4, step_in, lambda v: norm_act(v, gains[0:1]))
        times = (2, 1) if f == 0 else (2,)
        for start in range(0, rows + 2, step_one):
            part = pl.ds(start * pitch, step_one * pitch)
            fresh = product(taps_one, start, step_one, kernel_of(0, *times))
            hidden = sum_one[f, part] + fresh[:, :channels]
            if f == 0:
                sum_one[1, part] += fresh[:, channels:]
            put_taps(taps_two, start * pitch, norm_act(hidden, gains[1:2]) * inside[part])
        for start in range(0, rows, step_two):
            part = pl.ds(start * pitch, step_two * pitch)
            fresh = product(taps_two, start, step_two, kernel_of(1, *times))
            branch = sum_two[f, part] + fresh[:, :channels]
            if f == 0:
                sum_two[1, part] += fresh[:, channels:]
            branch = branch.reshape(step_two, pitch, channels)[:, STRIP : STRIP + cols]
            inputs = x_pad[f, 2 + start : 2 + start + step_two, STRIP : STRIP + cols]
            out[f, start : start + step_two] = (inputs.astype(jnp.float32) + branch).astype(out.dtype)
        each(onward[f], more, "start")

    for stream in streams[:2]:
        each(stream, None, "send")
    for f in range(total):
        each(streams[2 + f], first, "send")
        each(onward[f], more, "send")


def solution(mesh):
    counts = tuple(mesh.shape[name] for name in ("segment", "row", "col"))

    def on_device(frames, caches, weights, biases, gains):
        total, rows, cols, channels = frames.shape
        pitch = -(-(cols + 2 * STRIP) // 16) * 16
        bf16, f32 = jnp.bfloat16, jnp.float32
        vmem = pl.BlockSpec(memory_space=pltpu.VMEM)
        taps = weights.reshape(2, TAPS, TAPS * TAPS * channels, channels)
        result = pl.pallas_call(
            functools.partial(kernel, counts),
            out_shape=jax.ShapeDtypeStruct(frames.shape, bf16),
            in_specs=[vmem] * 5,
            out_specs=vmem,
            scratch_shapes=[
                pltpu.VMEM((total, rows + 4, pitch, channels), bf16),
                pltpu.VMEM((2, rows + 4, pitch, channels), bf16),
                pltpu.VMEM((2, rows + 2, pitch, channels), bf16),
                pltpu.VMEM(((rows + 4) * pitch, TAPS * channels), bf16),
                pltpu.VMEM(((rows + 2) * pitch, TAPS * channels), bf16),
                pltpu.VMEM((total, (rows + 2) * pitch, channels), f32),
                pltpu.VMEM((total, rows * pitch, channels), f32),
                pltpu.VMEM(((rows + 2) * pitch, channels), f32),
                pltpu.SemaphoreType.DMA((2 + 2 * total, 9)),
                pltpu.SemaphoreType.DMA((2 + total, 9)),
                pltpu.SemaphoreType.DMA((3,)),
            ],
            compiler_params=pltpu.CompilerParams(collective_id=0, has_side_effects=True),
        )(frames, caches[0], taps, biases[0], gains[0])
        return result[None]

    in_specs = (
        P(None, "row", "col", None),
        P("segment", None, None, "row", "col", None),
        P("segment", None, None, None, None, None, None),
        P("segment", None, None),
        P("segment", None, None),
    )
    out_specs = P("segment", None, "row", "col", None)
    return jax.shard_map(
        on_device, mesh=mesh, in_specs=in_specs, out_specs=out_specs, check_vma=False
    )
```

time: 158 us -> 35.3 us (0.22)
  the two profiles are of different devices: /device:TPU:25 before, /device:TPU:29 now
where the time goes in v1:
time: 35.3 us; the launch traced here: 34.9 us
  Pallas kernels  33.3 us (94%)
  local copies, waits for them, and re-layouts  1.57 us (4%)
    pallas_call x1, Pallas kernels, on_device(): pl.pallas_call(functools.partial(kernel, counts), out_shape=jax.ShapeDtyp...  33.3 us
    unnamed x1, local copies, waits for them, and re-layouts  1.57 us

profile of v1, /device:TPU:29, one launch (start us, length us, event | category | flops | bytes accessed | tf_op | source)
XLA Modules:
  0.0 34.9 jit_solution(1244660603647559176)
XLA Ops:
  0.0 33.3 %shard_map.55 = bf16[2,16,16,128]{3,2,1,0:T(8,128)(2,1)} custom-call(bf16[2,16,16,128]{3,2,1,0:T(8,128)(2,1)} %frames.1, bf16[2,2,16,16,128]{4,3,2,1,0:T(8,128)(2,1)} %bitcast.7, bf16[2,3,1152,128]{3,2,1,0:T(8,128)(2,1)} %bitcast.5, f32[2,128]{1,0:T(2,128)} %bitcast.8, f32[2,128]{1,0:T(2,128)} %bitcast.9), custom_call_target="tpu_custom_call" | custom-call | tf_op jit(solution)/shard_map/pallas_call | solution.py:237
  33.3 1.6 %copy.7 = bf16[1,2,16,16,128]{4,3,2,1,0:T(8,128)(2,1)} copy(bf16[1,2,16,16,128]{4,3,2,1,0:T(8,128)(2,1)} %bitcast.6) | data formatting | bytes 262144

commit v2 on v1

--- a/solution.py
+++ b/solution.py
@@ -7,7 +7,8 @@
 from jax.experimental.pallas import tpu as pltpu
 from jax.sharding import PartitionSpec as P
 
-STRIP = 8
+EDGE = 8
+STRIP = 2
 TAPS = 3
 AROUND = [(dr, dc) for dr in (-1, 0, 1) for dc in (-1, 0, 1)]
 CENTRE = AROUND.index((0, 0))
@@ -17,8 +18,10 @@
     return max(d for d in range(1, most + 1) if count % d == 0)
 
 
-def source_range(step, size, width):
-    return pl.ds(0, size) if step == 0 else pl.ds(0 if step < 0 else size - width, width)
+def source_range(step, size, width, edge):
+    if step == 0:
+        return pl.ds(edge, size)
+    return pl.ds(edge if step < 0 else edge + size - width, width)
 
 
 def target_range(step, size, width, edge):
@@ -43,9 +46,9 @@
 
 def kernel(
     counts,
-    frames, caches, weights, biases, gains,
+    frames, caches, weights_in, biases_in, gains_in,
     out,
-    x_pad, one_pad, two_pad, taps_one, taps_two, sum_one, sum_two, inside,
+    weights, biases, gains, x_pad, one_pad, two_pad, taps_one, taps_two, sum_one, sum_two, inside,
     send_sem, recv_sem, local_sem,
 ):
     segments, tile_rows_n, tile_cols_n = counts
@@ -62,8 +65,9 @@
 
     def remote(source, target, halo, send_group, recv_group, dz, which):
         dr, dc = AROUND[which]
-        src_r, src_c = source_range(dr, rows, halo), source_range(dc, cols, STRIP)
-        dst_r, dst_c = target_range(dr, rows, halo, halo), target_range(dc, cols, STRIP, STRIP)
+        top, left = (0, 0) if dz else (halo, EDGE)
+        src_r, src_c = source_range(dr, rows, halo, top), source_range(dc, cols, STRIP, left)
+        dst_r, dst_c = target_range(dr, rows, halo, halo), target_range(dc, cols, STRIP, EDGE)
         lead = (slice(None),) * (len(source.shape) - 3)
         return pltpu.make_async_remote_copy(
             src_ref=source.at[lead + (src_r, src_c)],
@@ -75,9 +79,9 @@
         )
 
     streams = [
-        (caches.at[0], one_pad, 2, 0, 0, 0),
-        (caches.at[1], two_pad, 1, 1, 1, 0),
-    ] + [(frames.at[f], x_pad.at[f], 2, 2 + f, 2 + f, 0) for f in range(total)]
+        (one_pad, one_pad, 2, 0, 0, 0),
+        (two_pad, two_pad, 1, 1, 1, 0),
+    ] + [(x_pad.at[f], x_pad.at[f], 2, 2 + f, 2 + f, 0) for f in range(total)]
     onward = [(out.at[f], x_pad.at[f], 2, 2 + total + f, 2 + f, 1) for f in range(total)]
 
     def each(stream, allowed, action):
@@ -98,13 +102,34 @@
                 else:
                     copy.wait_recv()
 
+    centre_of = lambda pad, halo: pad.at[:, pl.ds(halo, rows), pl.ds(EDGE, cols)]
+    first = seg == 0
+    later = seg > 0
+    more = seg < segments - 1
+    own = pltpu.make_async_copy(frames, centre_of(x_pad, 2), local_sem.at[0])
+    held_one = pltpu.make_async_copy(caches.at[0], centre_of(one_pad, 2), local_sem.at[1])
+    held_two = pltpu.make_async_copy(caches.at[1], centre_of(two_pad, 1), local_sem.at[2])
+    parameters = [
+        pltpu.make_async_copy(biases_in, biases, local_sem.at[3]),
+        pltpu.make_async_copy(gains_in, gains, local_sem.at[4]),
+        pltpu.make_async_copy(weights_in.at[0], weights.at[0], local_sem.at[5]),
+        pltpu.make_async_copy(weights_in.at[1], weights.at[1], local_sem.at[6]),
+    ]
+
+    @pl.when(first)
+    def _():
+        own.start()
+
+    for copy in [held_one, held_two] + parameters:
+        copy.start()
+
     for pad, halo in ((x_pad, 2), (one_pad, 2), (two_pad, 1)):
         count = pad.shape[0]
-        side = pitch - STRIP - cols
+        side = pitch - EDGE - cols
         pad[:, 0:halo] = jnp.zeros((count, halo, pitch, channels), pad.dtype)
         pad[:, halo + rows :] = jnp.zeros((count, halo, pitch, channels), pad.dtype)
-        pad[:, halo : halo + rows, 0:STRIP] = jnp.zeros((count, rows, STRIP, channels), pad.dtype)
-        pad[:, halo : halo + rows, STRIP + cols :] = jnp.zeros((count, rows, side, channels), pad.dtype)
+        pad[:, halo : halo + rows, 0:EDGE] = jnp.zeros((count, rows, EDGE, channels), pad.dtype)
+        pad[:, halo : halo + rows, EDGE + cols :] = jnp.zeros((count, rows, side, channels), pad.dtype)
 
     barrier = pltpu.get_barrier_semaphore()
     arrivals = 0
@@ -122,32 +147,22 @@
                 )
 
             arrivals = arrivals + good.astype(jnp.int32)
-    centre_of = lambda pad, halo: pad.at[:, pl.ds(halo, rows), pl.ds(STRIP, cols)]
-    local = [
-        pltpu.make_async_copy(caches.at[0], centre_of(one_pad, 2), local_sem.at[0]),
-        pltpu.make_async_copy(caches.at[1], centre_of(two_pad, 1), local_sem.at[1]),
-    ]
-    own = pltpu.make_async_copy(frames, centre_of(x_pad, 2), local_sem.at[2])
-    for copy in local:
-        copy.start()
-    first = seg == 0
-    later = seg > 0
-    more = seg < segments - 1
+    pl.semaphore_wait(barrier, arrivals)
 
     @pl.when(first)
     def _():
-        own.start()
-
-    pl.semaphore_wait(barrier, arrivals)
-
-    each(streams[0], None, "start")
+        own.wait()
+
     for f in range(total):
         each(streams[2 + f], first, "start")
+    held_one.wait()
+    each(streams[0], None, "start")
+    held_two.wait()
     each(streams[1], None, "start")
 
     cell = lax.broadcasted_iota(jnp.int32, inside.shape, 0)
     cell_row = row * rows + cell // pitch - 1
-    cell_col = col * cols + cell % pitch - STRIP
+    cell_col = col * cols + cell % pitch - EDGE
     inside[...] = jnp.where(
         (cell_row >= 0) & (cell_row < rows * tile_rows_n)
         & (cell_col >= 0) & (cell_col < cols * tile_cols_n), 1.0, 0.0,
@@ -184,16 +199,12 @@
             sums[0, part] += both[:, :channels]
             sums[1, part] = both[:, channels:] + bias
 
-    local[0].wait()
+    for copy in parameters:
+        copy.wait()
     each(streams[0], None, "recv")
     cached(0, one_pad, taps_one, sum_one, rows + 2, step_one, rows + 4)
-    local[1].wait()
     each(streams[1], None, "recv")
     cached(1, two_pad, taps_two, sum_two, rows, step_two, rows + 2)
-
-    @pl.when(first)
-    def _():
-        own.wait()
 
     for f in range(total):
         each(streams[2 + f], first, "recv")
@@ -213,8 +224,8 @@
             branch = sum_two[f, part] + fresh[:, :channels]
             if f == 0:
                 sum_two[1, part] += fresh[:, channels:]
-            branch = branch.reshape(step_two, pitch, channels)[:, STRIP : STRIP + cols]
-            inputs = x_pad[f, 2 + start : 2 + start + step_two, STRIP : STRIP + cols]
+            branch = branch.reshape(step_two, pitch, channels)[:, EDGE : EDGE + cols]
+            inputs = x_pad[f, 2 + start : 2 + start + step_two, EDGE : EDGE + cols]
             out[f, start : start + step_two] = (inputs.astype(jnp.float32) + branch).astype(out.dtype)
         each(onward[f], more, "start")
 
@@ -230,16 +241,19 @@
 
     def on_device(frames, caches, weights, biases, gains):
         total, rows, cols, channels = frames.shape
-        pitch = -(-(cols + 2 * STRIP) // 16) * 16
+        pitch = -(-(cols + 2 * EDGE) // 16) * 16
         bf16, f32 = jnp.bfloat16, jnp.float32
         vmem = pl.BlockSpec(memory_space=pltpu.VMEM)
         taps = weights.reshape(2, TAPS, TAPS * TAPS * channels, channels)
         result = pl.pallas_call(
             functools.partial(kernel, counts),
-            out_shape=jax.ShapeDtypeStruct(frames.shape, bf16),
-            in_specs=[vmem] * 5,
+            out_shape=pltpu.VMEM(frames.shape, bf16),
+            in_specs=[pl.BlockSpec(memory_space=pl.ANY)] * 5,
             out_specs=vmem,
             scratch_shapes=[
+                pltpu.VMEM(taps.shape, bf16),
+                pltpu.VMEM(biases.shape[1:], f32),
+                pltpu.VMEM(gains.shape[1:], f32),
                 pltpu.VMEM((total, rows + 4, pitch, channels), bf16),
                 pltpu.VMEM((2, rows + 4, pitch, channels), bf16),
                 pltpu.VMEM((2, rows + 2, pitch, channels), bf16),
@@ -250,7 +264,7 @@
                 pltpu.VMEM(((rows + 2) * pitch, channels), f32),
                 pltpu.SemaphoreType.DMA((2 + 2 * total, 9)),
                 pltpu.SemaphoreType.DMA((2 + total, 9)),
-                pltpu.SemaphoreType.DMA((3,)),
+                pltpu.SemaphoreType.DMA((7,)),
             ],
             compiler_params=pltpu.CompilerParams(collective_id=0, has_side_effects=True),
         )(frames, caches[0], taps, biases[0], gains[0])

time: 35.3 us -> 30 us (0.85)
  Pallas kernels: 33.3 us -> 29.2 us
  local copies, waits for them, and re-layouts: 1.57 us -> 0.66 us
    pallas_call x1, Pallas kernels: 33.3 us -> 29.2 us  [on_device(): pl.pallas_call(functools.partial(kernel, counts), out_shape=pltpu.VMEM(fr...]
    unnamed x1, local copies, waits for them, and re-layouts: 1.57 us -> 0.66 us
where the time goes in v2:
time: 30 us; the launch traced here: 29.9 us
  Pallas kernels  29.2 us (97%)
  local copies, waits for them, and re-layouts  0.66 us (2%)
    pallas_call x1, Pallas kernels, on_device(): pl.pallas_call(functools.partial(kernel, counts), out_shape=pltpu.VMEM(fr...  29.2 us
    unnamed x1, local copies, waits for them, and re-layouts  0.66 us

profile of v2, /device:TPU:29, one launch (start us, length us, event | category | flops | bytes accessed | tf_op | source)
XLA Modules:
  0.0 29.9 jit_solution(9941189470084353788)
XLA Ops:
  0.0 29.2 %shard_map.55 = bf16[2,16,16,128]{3,2,1,0:T(8,128)(2,1)S(1)} custom-call(bf16[2,16,16,128]{3,2,1,0:T(8,128)(2,1)} %frames.1, bf16[2,2,16,16,128]{4,3,2,1,0:T(8,128)(2,1)} %bitcast.7, bf16[2,3,1152,128]{3,2,1,0:T(8,128)(2,1)} %bitcast.6, f32[2,128]{1,0:T(2,128)} %bitcast.8, f32[2,128]{1,0:T(2,128)} %bitcast.9), custom_call_target="tpu_custom_call" | custom-call | tf_op jit(solution)/shard_map/pallas_call | solution.py:248
  29.2 0.7 %copy.7 = bf16[1,2,16,16,128]{4,3,2,1,0:T(8,128)(2,1)} copy(bf16[1,2,16,16,128]{4,3,2,1,0:T(8,128)(2,1)S(1)} %bitcast.5) | data formatting | bytes 262144

commit v3 on v2

--- a/solution.py
+++ b/solution.py
@@ -10,7 +10,7 @@
 EDGE = 8
 STRIP = 2
 TAPS = 3
-AROUND = [(dr, dc) for dr in (-1, 0, 1) for dc in (-1, 0, 1)]
+AROUND = [(dr, dc) for dr in (-1, 1, 0) for dc in (-1, 1, 0)]
 CENTRE = AROUND.index((0, 0))
 
 
@@ -48,8 +48,9 @@
     counts,
     frames, caches, weights_in, biases_in, gains_in,
     out,
-    weights, biases, gains, x_pad, one_pad, two_pad, taps_one, taps_two, sum_one, sum_two, inside,
-    send_sem, recv_sem, local_sem,
+    weights, biases, gains, x_pad, one_pad, two_pad, taps_one, taps_two,
+    held_taps_one, held_taps_two, sum_one, sum_two, inside,
+    send_sem, recv_sem, tile_send, tile_recv, local_sem,
 ):
     segments, tile_rows_n, tile_cols_n = counts
     seg, row, col = (lax.axis_index(name) for name in ("segment", "row", "col"))
@@ -84,9 +85,25 @@
     ] + [(x_pad.at[f], x_pad.at[f], 2, 2 + f, 2 + f, 0) for f in range(total)]
     onward = [(out.at[f], x_pad.at[f], 2, 2 + total + f, 2 + f, 1) for f in range(total)]
 
-    def each(stream, allowed, action):
+    step_in = divisor(rows + 4, 5)
+    step_one = divisor(rows + 2, 6)
+    step_two = divisor(rows, 4)
+    chunks = rows // step_two
+
+    def tile_copy(f, chunk):
+        start = chunk * step_two
+        return pltpu.make_async_remote_copy(
+            src_ref=out.at[f, pl.ds(start, step_two)],
+            dst_ref=x_pad.at[f, pl.ds(2 + start, step_two), pl.ds(EDGE, cols)],
+            send_sem=tile_send.at[f, chunk],
+            recv_sem=tile_recv.at[f, chunk],
+            device_id=device(1, 0, 0),
+            device_id_type=pl.DeviceIdType.MESH,
+        )
+
+    def each(stream, allowed, action, steps=(-1, 1, 0)):
         for which, (dr, dc) in enumerate(AROUND):
-            if stream[5] == 0 and which == CENTRE:
+            if which == CENTRE or dr not in steps:
                 continue
             good = exists(dr, dc) if action != "recv" else exists(-dr, -dc)
             if allowed is not None:
@@ -177,38 +194,52 @@
         )
         return jnp.dot(patches, matrix, preferred_element_type=jnp.float32)
 
-    step_in = divisor(rows + 4, 5)
-    step_one = divisor(rows + 2, 6)
-    step_two = divisor(rows, 4)
-
     def load_taps(pad, index, store, size, step, transform):
         for start in range(0, size, step):
             values = pad[index, start : start + step].reshape(step * pitch, channels)
             put_taps(store, start * pitch, transform(values.astype(jnp.float32)))
 
-    def cached(which, pad, store, sums, size, step, tall):
+    def cached(which, pad, store, sums, tap_rows, sum_rows):
         bias = biases[which : which + 1]
-        load_taps(pad, 0, store, tall, divisor(tall, 5), lambda v: v)
-        for start in range(0, size, step):
-            part = pl.ds(start * pitch, step * pitch)
-            sums[0, part] = product(store, start, step, kernel_of(which, 0)) + bias
-        load_taps(pad, 1, store, tall, divisor(tall, 5), lambda v: v)
-        for start in range(0, size, step):
-            part = pl.ds(start * pitch, step * pitch)
-            both = product(store, start, step, kernel_of(which, 1, 0))
-            sums[0, part] += both[:, :channels]
-            sums[1, part] = both[:, channels:] + bias
+        for frame in range(2):
+            for low, high in tap_rows:
+                step = divisor(high - low, 4)
+                for start in range(low, high, step):
+                    values = pad[frame, start : start + step].reshape(step * pitch, channels)
+                    put_taps(store.at[frame], start * pitch, values.astype(jnp.float32))
+        for low, high in sum_rows:
+            step = divisor(high - low, 7)
+            for start in range(low, high, step):
+                part = pl.ds(start * pitch, step * pitch)
+                older = product(store.at[0], start, step, kernel_of(which, 0))
+                newer = product(store.at[1], start, step, kernel_of(which, 1, 0))
+                sums[0, part] = older + newer[:, :channels] + bias
+                sums[1, part] = newer[:, channels:] + bias
 
     for copy in parameters:
         copy.wait()
-    each(streams[0], None, "recv")
-    cached(0, one_pad, taps_one, sum_one, rows + 2, step_one, rows + 4)
-    each(streams[1], None, "recv")
-    cached(1, two_pad, taps_two, sum_two, rows, step_two, rows + 2)
+    held = ((one_pad, held_taps_one, sum_one, 2), (two_pad, held_taps_two, sum_two, 1))
+    for which, (pad, store, sums, halo) in enumerate(held):
+        end = halo + rows
+        each(streams[which], None, "recv", (0,))
+        cached(which, pad, store, sums, [(halo, end)], [(halo, end - 2)])
+    for which, (pad, store, sums, halo) in enumerate(held):
+        end = halo + rows
+        each(streams[which], None, "recv", (-1, 1))
+        cached(
+            which, pad, store, sums,
+            [(0, halo), (end, end + halo)], [(0, halo), (end - 2, end + halo - 2)],
+        )
 
     for f in range(total):
         each(streams[2 + f], first, "recv")
         each(onward[f], later, "recv")
+
+        @pl.when(later)
+        def _():
+            for chunk in range(chunks):
+                tile_copy(f, chunk).wait_recv()
+
         load_taps(x_pad, f, taps_one, rows + 4, step_in, lambda v: norm_act(v, gains[0:1]))
         times = (2, 1) if f == 0 else (2,)
         for start in range(0, rows + 2, step_one):
@@ -218,7 +249,8 @@
             if f == 0:
                 sum_one[1, part] += fresh[:, channels:]
             put_taps(taps_two, start * pitch, norm_act(hidden, gains[1:2]) * inside[part])
-        for start in range(0, rows, step_two):
+        for chunk in [0, chunks - 1] + list(range(1, chunks - 1)) if chunks > 1 else [0]:
+            start = chunk * step_two
             part = pl.ds(start * pitch, step_two * pitch)
             fresh = product(taps_two, start, step_two, kernel_of(1, *times))
             branch = sum_two[f, part] + fresh[:, :channels]
@@ -227,13 +259,27 @@
             branch = branch.reshape(step_two, pitch, channels)[:, EDGE : EDGE + cols]
             inputs = x_pad[f, 2 + start : 2 + start + step_two, EDGE : EDGE + cols]
             out[f, start : start + step_two] = (inputs.astype(jnp.float32) + branch).astype(out.dtype)
-        each(onward[f], more, "start")
+            if chunk == 0:
+                each(onward[f], more, "start", (-1,))
+            if chunk == chunks - 1:
+                each(onward[f], more, "start", (1,))
+
+            @pl.when(more)
+            def _():
+                tile_copy(f, chunk).start()
+
+        each(onward[f], more, "start", (0,))
 
     for stream in streams[:2]:
         each(stream, None, "send")
     for f in range(total):
         each(streams[2 + f], first, "send")
         each(onward[f], more, "send")
+
+        @pl.when(more)
+        def _():
+            for chunk in range(chunks):
+                tile_copy(f, chunk).wait_send()
 
 
 def solution(mesh):
@@ -259,11 +305,15 @@
                 pltpu.VMEM((2, rows + 2, pitch, channels), bf16),
                 pltpu.VMEM(((rows + 4) * pitch, TAPS * channels), bf16),
                 pltpu.VMEM(((rows + 2) * pitch, TAPS * channels), bf16),
+                pltpu.VMEM((2, (rows + 4) * pitch, TAPS * channels), bf16),
+                pltpu.VMEM((2, (rows + 2) * pitch, TAPS * channels), bf16),
                 pltpu.VMEM((total, (rows + 2) * pitch, channels), f32),
                 pltpu.VMEM((total, rows * pitch, channels), f32),
                 pltpu.VMEM(((rows + 2) * pitch, channels), f32),
                 pltpu.SemaphoreType.DMA((2 + 2 * total, 9)),
                 pltpu.SemaphoreType.DMA((2 + total, 9)),
+                pltpu.SemaphoreType.DMA((total, divisor(rows, 16))),
+                pltpu.SemaphoreType.DMA((total, divisor(rows, 16))),
                 pltpu.SemaphoreType.DMA((7,)),
             ],
             compiler_params=pltpu.CompilerParams(collective_id=0, has_side_effects=True),

time: 30 us -> 27.5 us (0.917)
  Pallas kernels: 29.2 us -> 26.7 us
    pallas_call x1, Pallas kernels: 29.2 us -> 26.7 us  [on_device(): pl.pallas_call(functools.partial(kernel, counts), out_shape=pltpu.VMEM(fr...]
where the time goes in v3:
time: 27.5 us; the launch traced here: 27.3 us
  Pallas kernels  26.7 us (97%)
  local copies, waits for them, and re-layouts  0.66 us (2%)
    pallas_call x1, Pallas kernels, on_device(): pl.pallas_call(functools.partial(kernel, counts), out_shape=pltpu.VMEM(fr...  26.7 us
    unnamed x1, local copies, waits for them, and re-layouts  0.66 us

profile of v3, /device:TPU:29, one launch (start us, length us, event | category | flops | bytes accessed | tf_op | source)
XLA Modules:
  0.0 27.3 jit_solution(3995826039751870974)
XLA Ops:
  0.0 26.7 %shard_map.55 = bf16[2,16,16,128]{3,2,1,0:T(8,128)(2,1)S(1)} custom-call(bf16[2,16,16,128]{3,2,1,0:T(8,128)(2,1)} %frames.1, bf16[2,2,16,16,128]{4,3,2,1,0:T(8,128)(2,1)} %bitcast.7, bf16[2,3,1152,128]{3,2,1,0:T(8,128)(2,1)} %bitcast.6, f32[2,128]{1,0:T(2,128)} %bitcast.8, f32[2,128]{1,0:T(2,128)} %bitcast.9), custom_call_target="tpu_custom_call" | custom-call | tf_op jit(solution)/shard_map/pallas_call | solution.py:294
  26.7 0.7 %copy.7 = bf16[1,2,16,16,128]{4,3,2,1,0:T(8,128)(2,1)} copy(bf16[1,2,16,16,128]{4,3,2,1,0:T(8,128)(2,1)S(1)} %bitcast.5) | data formatting | bytes 262144
